TPU v7x, 1024 devices: a whole 8x8x8 slice. The times are simulated.
1024 devices in a mesh: expert: 8 (over x), dp: 8 (over z_lo, core), mp: 16 (over z_hi, y).
Axes of the slice: x: 8, y: 8, z: 8 (z_hi: 2, z_lo: 4; z = z_hi * 4 + z_lo), core: 2. Of those that a mesh axis runs over, the one named last changes fastest.
Arguments:
- tokens: bfloat16 [768, 4096], P(('expert', 'dp'), 'mp'), may hold values from -6 to 6
- routes: int32 [768, 2], P(('expert', 'dp')), may hold values from 0 to 7, all different within a row; in each aligned block of 12 rows (0 to 11, 12 to 23, ...) at most 5 rows name the same one
- router_weight: bfloat16 [4096, 8], P('mp'), may hold values from -0.09375 to 0.09375
- gate_weight: bfloat16 [8, 4096, 16384], P('expert', None, ('dp', 'mp')), may hold values from -0.09375 to 0.09375
- up_weight: bfloat16 [8, 4096, 16384], P('expert', None, ('dp', 'mp')), may hold values from -0.09375 to 0.09375
- down_weight: bfloat16 [8, 16384, 4096], P('expert', ('dp', 'mp')), may hold values from -0.1875 to 0.1875
Outputs:
- mixed: bfloat16 [768, 4096], P(('expert', 'dp'), 'mp')
Inputs may be any that keep to these rules, and one draw needn't show every extreme that they name: `routes`: each row names two different experts; among the 12 rows of one device (aligned blocks) no expert is named more than 5 times, a bound that some block reaches.
All inputs are finite; a program needn't handle non-finite values.
Results may differ from a plain program's by a relative error of at most 0.0049.
Values may be sent and summed in bfloat16 or wider, within the bound.
A program may use at most 32 MiB of HBM per device.

v0:
```python
import jax
import jax.numpy as jnp
from jax import lax
from jax.sharding import PartitionSpec as P


def from_everyone(x, axis):
    length = lax.axis_size(axis)
    return lax.all_to_all(jnp.broadcast_to(x[None], (length, *x.shape)), axis, 0, 0, tiled=True)


def over_copies(x, axis):
    everything = from_everyone(x, axis)
    return jnp.sum(everything, axis=0)


def joined_along(pieces, dim):
    lengths = list(pieces.shape[1:])
    lengths[dim] *= pieces.shape[0]
    return jnp.moveaxis(pieces, 0, dim).reshape(lengths)


def gathered_copies(x, axis, dim):
    pieces = from_everyone(x, axis)
    return joined_along(pieces, dim)


def in_blocks(x, dim, length):
    before, after = (x.shape[:dim], x.shape[dim + 1 :])
    return jnp.moveaxis(x.reshape(*before, length, -1, *after), dim, 0)


def summed_on_arrival(x, axis, dim):
    length = lax.axis_size(axis)
    pieces = lax.all_to_all(in_blocks(x, dim, length), axis, 0, 0, tiled=True)
    return jnp.sum(pieces, axis=0)


def per_device(tokens, routes, router_weight, gate_weight, up_weight, down_weight):
    row_count = tokens.shape[0]
    experts = lax.axis_size("expert")
    capacity = max(2, (6 * row_count + 2 * experts - 1) // (2 * experts))
    partial_logits = jnp.dot(tokens, router_weight, preferred_element_type=jnp.float32)
    logits = over_copies(partial_logits, "mp")
    labels = jnp.arange(experts, dtype=jnp.int32)
    onehot = (routes[:, :, None] == labels).astype(jnp.int32)
    chosen = jnp.sum(onehot.astype(jnp.float32) * logits[:, None, :], axis=2)
    weights = jnp.stack(
        [jax.nn.sigmoid(chosen[:, 0] - chosen[:, 1]), jax.nn.sigmoid(chosen[:, 1] - chosen[:, 0])],
        axis=1,
    )
    flat_hot = onehot.reshape(row_count * 2, experts)
    before = jnp.cumsum(flat_hot, axis=0) - flat_hot
    position = jnp.sum(flat_hot * before, axis=1)
    places = (position[:, None] == jnp.arange(capacity, dtype=jnp.int32)).astype(jnp.float32)
    assign = (flat_hot.astype(jnp.float32)[:, :, None] * places[:, None, :]).reshape(
        row_count, 2, experts, capacity
    )
    select = jnp.sum(assign, axis=1).astype(jnp.bfloat16)
    combine = jnp.sum(assign * weights[:, :, None, None], axis=1).reshape(
        row_count, experts * capacity
    )
    full_rows = gathered_copies(tokens, "mp", 1)
    full_width = full_rows.shape[1]
    buffer = jnp.einsum(
        "tec,td->ecd", select, full_rows, preferred_element_type=jnp.float32
    ).astype(jnp.bfloat16)
    arrived = lax.all_to_all(buffer, "expert", split_axis=0, concat_axis=0, tiled=True)
    inputs = lax.all_gather(
        arrived.reshape(experts * capacity, full_width), "dp", axis=0, tiled=True
    )
    gate_part = jnp.dot(inputs, gate_weight[0], preferred_element_type=jnp.float32)
    up_part = jnp.dot(inputs, up_weight[0], preferred_element_type=jnp.float32)
    hidden = (jax.nn.silu(gate_part) * up_part).astype(jnp.bfloat16)
    summed = lax.psum_scatter(
        jnp.dot(hidden, down_weight[0], preferred_element_type=jnp.float32),
        "dp",
        scatter_dimension=0,
        tiled=True,
    )
    returned = lax.all_to_all(
        summed.reshape(experts, capacity, full_width),
        "expert",
        split_axis=0,
        concat_axis=0,
        tiled=True,
    )
    partial_mix = jnp.dot(
        combine,
        returned.reshape(experts * capacity, full_width),
        precision=lax.Precision.HIGHEST,
        preferred_element_type=jnp.float32,
    )
    mixed_out = summed_on_arrival(partial_mix, "mp", 1)
    return mixed_out.astype(jnp.bfloat16)


def solution(mesh):
    return jax.shard_map(
        per_device,
        mesh=mesh,
        in_specs=(
            P(("expert", "dp"), "mp"),
            P(("expert", "dp"), None),
            P("mp", None),
            P("expert", None, ("dp", "mp")),
            P("expert", None, ("dp", "mp")),
            P("expert", ("dp", "mp"), None),
        ),
        out_specs=P(("expert", "dp"), "mp"),
        check_vma=False,
    )
```

profile of v0, /device:TPU:1, one launch (start us, length us, event | category | flops | bytes accessed | tf_op | source)
XLA Modules:
  0.0 270.6 jit_solution(13023815464682987491)
XLA Ops:
  6.5 0.0 copy-start
  6.5 0.9 fusion.20
  7.4 0.6 broadcast_in_dim.4
  8.1 20.3 %all-to-all-start = ((f32[16,12,8]{1,2,0:T(8,128)}), f32[16,12,8]{1,2,0:T(8,128)S(1)}, u32[]{:S(2)}, u32[]{:S(2)}) async-start(f32[16,12,8]{1,2,0:T(8,128)} %broadcast_in_dim.4), calls=%async_computation | async-start | bytes 131072 | tf_op jit(solution)/shard_map/all_to_all | solution.py:9
  28.4 0.8 copy.31
  29.1 0.7 convert_convert_fusion
  29.8 0.1 eq.48
  29.9 0.1 fusion.16
  30.0 0.2 select_reduce_fusion
  30.2 0.1 eq.52
  30.3 0.1 copy.32
  30.4 9.3 %all-to-all-done = f32[16,12,8]{1,2,0:T(8,128)S(1)} async-done(((f32[16,12,8]{1,2,0:T(8,128)}), f32[16,12,8]{1,2,0:T(8,128)S(1)}, u32[]{:S(2)}, u32[]{:S(2)}) %all-to-all-start) | async-done | bytes 6176 | tf_op jit(solution)/shard_map/all_to_all | solution.py:9
  39.6 1.3 broadcast_in_dim.5
  41.0 3.5 %all-to-all-start.1 = ((bf16[16,12,256]{2,1,0:T(8,128)(2,1)}), bf16[16,12,256]{2,1,0:T(8,128)(2,1)S(1)}, u32[]{:S(2)}, u32[]{:S(2)}) async-start(bf16[16,12,256]{2,1,0:T(8,128)(2,1)} %broadcast_in_dim.5), calls=%async_computation.1 | async-start | bytes 262144 | tf_op jit(solution)/shard_map/all_to_all | solution.py:9
  44.5 0.0 all-gather.2.cloned.1.call-start
  44.6 0.7 multiply_reduce_fusion.1
  45.3 10.6 %all-to-all-done.1 = bf16[16,12,256]{2,1,0:T(8,128)(2,1)S(1)} async-done(((bf16[16,12,256]{2,1,0:T(8,128)(2,1)}), bf16[16,12,256]{2,1,0:T(8,128)(2,1)S(1)}, u32[]{:S(2)}, u32[]{:S(2)}) %all-to-all-start.1) | async-done | bytes 98336 | tf_op jit(solution)/shard_map/all_to_all | solution.py:9
  56.0 0.1 reshape.76
  56.1 0.2 convolution_convert_fusion
  56.3 0.2 copy.35
  56.5 19.4 %all_to_all.25 = bf16[8,5,4096]{2,1,0:T(8,128)(2,1)S(1)} all-to-all(bf16[8,5,4096]{2,1,0:T(8,128)(2,1)S(1)} %copy.35), channel_id=1, replica_groups=mesh['expert'=8,'dp'=8,'mp'=16] {'expert'}, dimensions={0} | all-to-all | bytes 655360 | tf_op jit(solution)/shard_map/all_to_all | solution.py:68
  75.9 0.0 copy-start.1
  75.9 0.9 reshape.73
  76.7 0.0 all-gather.2.cloned.1.call-update
  76.7 0.0 reduce-scatter.2.cloned.1.call-start
  76.8 42.5 %all-gather.2.cloned.1.call-done = bf16[320,4096]{1,0:T(8,128)(2,1)} async-done(((bf16[40,4096]{1,0:T(8,128)(2,1)}), bf16[320,4096]{1,0:T(8,128)(2,1)}) %all-gather.2.cloned.1.call-update) | async-done | bytes 2621456 | tf_op jit(solution)/shard_map/all_gather | solution.py:69
  119.3 2.9 %fusion.5 = f32[320,128]{1,0:T(8,128)S(1)} fusion(bf16[320,4096]{1,0:T(8,128)(2,1)} %all-gather.2.cloned.1.call-done, bf16[1,4096,128]{2,1,0:T(8,128)(2,1)} %param.9), kind=kOutput, calls=%fused_computation.7 | convolution fusion | flops 335544320 | bytes 3833856 | tf_op jit(solution)/shard_map/dot_general | solution.py:72
  122.1 0.0 copy-done
  122.2 0.0 copy-done.1
  122.2 7.0 %fusion.1 = f32[320,4096]{1,0:T(8,128)} fusion(bf16[320,4096]{1,0:T(8,128)(2,1)} %all-gather.2.cloned.1.call-done, bf16[1,128,4096]{2,1,0:T(8,128)(2,1)S(1)} %copy-done, bf16[1,4096,128]{2,1,0:T(8,128)(2,1)S(1)} %copy-done.1, f32[320,128]{1,0:T(8,128)S(1)} %fusion.5), kind=kOutput, calls=%fused_computation.4 | convolution fusion | flops 671334400 | bytes 10125312 | tf_op jit(solution)/shard_map/dot_general | solution.py:76
  129.1 0.0 reduce-scatter.2.cloned.1.call-update
  129.1 69.3 %reduce-scatter.2.cloned.1.call-done = f32[40,4096]{1,0:T(8,128)} async-done(((f32[320,4096]{1,0:T(8,128)}), f32[40,4096]{1,0:T(8,128)}) %reduce-scatter.2.cloned.1.call-update) | async-done | bytes 655376 | tf_op jit(solution)/shard_map/reduce_scatter | solution.py:75
  198.5 2.2 reshape.74
  200.6 6.4 %all-to-all-start.3 = ((f32[8,5,4096]{2,1,0:T(8,128)}), f32[8,5,4096]{2,1,0:T(8,128)S(1)}, u32[]{:S(2)}, u32[]{:S(2)}) async-start(f32[8,5,4096]{2,1,0:T(8,128)} %reshape.74), calls=%async_computation.4 | async-start | bytes 2097152 | tf_op jit(solution)/shard_map/all_to_all | solution.py:81
  207.1 25.7 %all-to-all-done.3 = f32[8,5,4096]{2,1,0:T(8,128)S(1)} async-done(((f32[8,5,4096]{2,1,0:T(8,128)}), f32[8,5,4096]{2,1,0:T(8,128)S(1)}, u32[]{:S(2)}, u32[]{:S(2)}) %all-to-all-start.3) | async-done | bytes 655392 | tf_op jit(solution)/shard_map/all_to_all | solution.py:81
  232.7 0.1 reshape.75
  232.9 0.5 convolution_bitcast_fusion
  233.4 29.8 %all_to_all.26 = f32[16,12,256]{2,1,0:T(8,128)S(1)} all-to-all(f32[16,12,256]{2,1,0:T(8,128)S(1)} %convolution_bitcast_fusion), channel_id=1, replica_groups=mesh['expert'=8,'dp'=8,'mp'=16] {'mp'}, dimensions={0} | all-to-all | bytes 393216 | tf_op jit(solution)/shard_map/all_to_all | solution.py:35
  263.2 0.6 reduce_sum.59
  (9 shorter events, 0.2 us)
Async XLA Ops:
  6.5 115.6 %copy-start = (bf16[1,128,4096]{2,1,0:T(8,128)(2,1)S(1)}, bf16[1,128,4096]{2,1,0:T(8,128)(2,1)}, u32[]{:S(2)}) copy-start(bf16[1,128,4096]{2,1,0:T(8,128)(2,1)} %param.11) | copy-start | bytes 3145732
  8.1 31.6 %all-to-all-start = ((f32[16,12,8]{1,2,0:T(8,128)}), f32[16,12,8]{1,2,0:T(8,128)S(1)}, u32[]{:S(2)}, u32[]{:S(2)}) async-start(f32[16,12,8]{1,2,0:T(8,128)} %broadcast_in_dim.4), calls=%async_computation | async-start | bytes 131072 | tf_op jit(solution)/shard_map/all_to_all | solution.py:9
  41.0 15.0 %all-to-all-start.1 = ((bf16[16,12,256]{2,1,0:T(8,128)(2,1)}), bf16[16,12,256]{2,1,0:T(8,128)(2,1)S(1)}, u32[]{:S(2)}, u32[]{:S(2)}) async-start(bf16[16,12,256]{2,1,0:T(8,128)(2,1)} %broadcast_in_dim.5), calls=%async_computation.1 | async-start | bytes 262144 | tf_op jit(solution)/shard_map/all_to_all | solution.py:9
  44.5 74.8 %all-gather.2.cloned.1.call-start = ((), (), s32[]{:S(2)}) async-start(), calls=%async_computation.6 | async-start | bytes 2949120 | tf_op jit(solution)/shard_map/all_gather | solution.py:69
  75.9 46.3 %copy-start.1 = (bf16[1,4096,128]{2,1,0:T(8,128)(2,1)S(1)}, bf16[1,4096,128]{2,1,0:T(8,128)(2,1)}, u32[]{:S(2)}) copy-start(bf16[1,4096,128]{2,1,0:T(8,128)(2,1)} %param.10) | copy-start | bytes 3145732
  76.7 121.7 %reduce-scatter.2.cloned.1.call-start = ((), (), s32[]{:S(2)}) async-start(), calls=%async_computation.7 | async-start | bytes 5898240 | tf_op jit(solution)/shard_map/reduce_scatter | solution.py:75
  200.6 32.1 %all-to-all-start.3 = ((f32[8,5,4096]{2,1,0:T(8,128)}), f32[8,5,4096]{2,1,0:T(8,128)S(1)}, u32[]{:S(2)}, u32[]{:S(2)}) async-start(f32[8,5,4096]{2,1,0:T(8,128)} %reshape.74), calls=%async_computation.4 | async-start | bytes 2097152 | tf_op jit(solution)/shard_map/all_to_all | solution.py:81
Sparse Core Ops, SparseCore 0:
  76.9 42.3 all-gather.1
  129.3 69.1 reduce-scatter.1
where the time goes:
time: 272 us; the launch traced here: 271 us
  waiting for transfers between devices  157 us (58%)
  blocking collectives  49.2 us (18%)
  starting transfers between devices  30.3 us (11%)
  between operations  13.5 us (5%)
  matrix products  11.4 us (4%)
  local copies, waits for them, and re-layouts  6.47 us (2%)
    reduce_scatter x1, waiting for transfers between devices, per_device(): lax.psum_scatter(jnp.dot(hidden, down_weight[0], preferred_element_type=j...  69.3 us
    all_gather x1, waiting for transfers between devices, per_device(): lax.all_gather(arrived.reshape(experts * capacity, full_width), 'dp', axi...  42.5 us
    all_to_all x1, blocking collectives, summed_on_arrival(): pieces = lax.all_to_all(in_blocks(x, dim, length), axis, 0, 0, tiled=True)  29.8 us
    all_to_all x1, waiting for transfers between devices, per_device(): lax.all_to_all(summed.reshape(experts, capacity, full_width), 'expert', s...  25.7 us
    all_to_all x2, starting transfers between devices, from_everyone(): lax.all_to_all(jnp.broadcast_to(x[None], (length, *x.shape)), axis, 0, 0,...  23.8 us
    all_to_all x2, waiting for transfers between devices, from_everyone(): lax.all_to_all(jnp.broadcast_to(x[None], (length, *x.shape)), axis, 0, 0,...  19.9 us
    all_to_all x1, blocking collectives, per_device(): lax.all_to_all(buffer, 'expert', split_axis=0, concat_axis=0, tiled=True)  19.4 us
    dot_general x1, matrix products, per_device(): jnp.dot(hidden, down_weight[0], preferred_element_type=jnp.float32)  6.95 us
  transfers between devices with their start and end apart: 5, of which 5 were waited for; matrix products, arithmetic and copies ran while one was open for 1% of the time, Pallas kernels for 0%

commit v1 on v0

v1 whole, which is shorter than its diff:
```python
import jax
import jax.numpy as jnp
from jax import lax
from jax.experimental import pallas as pl
from jax.experimental.pallas import tpu as pltpu
from jax.sharding import PartitionSpec as P

MESH = pl.DeviceIdType.MESH
F32 = jnp.float32
BF16 = jnp.bfloat16
RING = 8
TOK = 12
CAP = 5
SLOT = 8
ROWS = 2 * RING * CAP
LANES = 128


def iota(shape, dim):
    return lax.broadcasted_iota(jnp.int32, shape, dim)


def kernel(
    tokens, routes, router, gate, up, down, out,
    tx, rx, xg, wg, wu, wd, acc, peer, hid, long_out, short_out, long_in, short_in,
    last_out, last_in, back_out, back_in, fin, logit_y, logit_z, logit_far,
    weight_local, weight_send, weight_recv, x_send, x_recv, first_send, ring_send, gather_recv,
    logit_send, logit_recv, swap_send, swap_recv, reduce_send, long_recv, short_recv,
    last_send, last_recv, back_send, back_recv,
):
    x = lax.axis_index("expert")
    dp = lax.axis_index("dp")
    mp = lax.axis_index("mp")
    core = dp % 2
    z = (mp // RING) * 4 + dp // 2
    y = mp % RING
    a1 = (1 - core) * y + core * z
    a2 = (1 - core) * z + core * y

    def device(dx, dy, dz, dcore):
        return (dx, (dz % 4) * 2 + dcore, (dz // 4) * RING + dy)

    def turned(b1, b2):
        return (1 - core) * b1 + core * b2, (1 - core) * b2 + core * b1

    def on_plane(b1, b2):
        dy, dz = turned(b1, b2)
        return device(x, dy, dz, core)

    def send(src, dst, send_sem, recv_sem, target):
        pltpu.make_async_remote_copy(
            src_ref=src, dst_ref=dst, send_sem=send_sem, recv_sem=recv_sem,
            device_id=target, device_id_type=MESH,
        ).start()

    def wait(ref, sem):
        pltpu.make_async_copy(ref, ref, sem).wait()

    barrier = pltpu.get_barrier_semaphore()

    def greet(target):
        pl.semaphore_signal(barrier, inc=1, device_id=target, device_id_type=MESH)

    for d in (4, 3, 5, 2, 6, 1, 7):
        greet(device((x + d) % RING, y, z, core))
        greet(device((x + d) % RING, y, z, 1 - core))
        greet(device(x, (y + d) % RING, z, core))
        greet(device(x, y, (z + d) % RING, core))
    greet(device(x, y, z, 1 - core))

    pltpu.make_async_copy(
        gate.at[:, core], wg.at[:, :, pl.ds(pl.multiple_of(core * LANES, LANES), LANES)], weight_local.at[0]
    ).start()
    pltpu.make_async_copy(
        up.at[:, core], wu.at[:, :, pl.ds(pl.multiple_of(core * LANES, LANES), LANES)], weight_local.at[1]
    ).start()

    def down_columns(block, half):
        return down.at[:, pl.ds(pl.multiple_of((block * 2 + half) * LANES, LANES), LANES)]

    def down_rows(block):
        return wd.at[block, pl.ds(pl.multiple_of(core * LANES, LANES), LANES)]

    @pl.loop(0, 2 * RING)
    def _(block):
        pltpu.make_async_copy(down_columns(block, core), down_rows(block), weight_local.at[2]).start()

    r0 = routes[:, 0:1]
    r1 = routes[:, 1:2]
    lane = iota((TOK, LANES), 1)
    hot0 = r0 == lane // SLOT
    hot1 = r1 == lane // SLOT
    hot = jnp.where(hot0 | hot1, 1.0, 0.0)
    earlier = jnp.where(iota((TOK, TOK), 1) < iota((TOK, TOK), 0), 1.0, 0.0)
    before = jnp.dot(earlier.astype(BF16), hot.astype(BF16), preferred_element_type=F32)
    assign = jnp.where(before == (lane % SLOT).astype(F32), hot, 0.0)
    tok = tokens[...]
    chosen = lax.dot_general(
        assign.astype(BF16), tok, (((0,), (0,)), ((), ())), preferred_element_type=F32
    )
    for e in range(RING):
        for half in range(2):
            tx[e * 2 + half] = chosen[
                e * SLOT : (e + 1) * SLOT, half * LANES : (half + 1) * LANES
            ].astype(BF16)

    spread = jnp.where(iota((RING, LANES), 1) % RING == iota((RING, LANES), 0), 1.0, 0.0)
    router_wide = jnp.dot(router[...], spread.astype(BF16), preferred_element_type=F32).astype(BF16)
    term = jnp.dot(tok, router_wide, preferred_element_type=F32)
    own_lanes = lane // RING == iota((TOK, LANES), 0)
    logit_y[0] = jnp.sum(jnp.where(own_lanes, term, 0.0), axis=0, keepdims=True)
    acc[...] = jnp.zeros_like(acc)
    me_x = x * 2 + core
    rx[me_x] = tx[me_x]

    pl.semaphore_wait(barrier, 4 * (RING - 1) + 1)

    for d in (4, 3, 5, 2, 6, 1, 7, 0):
        e = (x + d) % RING
        send(tx.at[e * 2 + 1 - core], rx.at[me_x], x_send, x_recv, device(e, y, z, 1 - core))
        if d:
            send(tx.at[e * 2 + core], rx.at[me_x], x_send, x_recv, device(e, y, z, core))
    for d in (4, 3, 5, 2, 6, 1, 7):
        send(logit_y.at[0], logit_y.at[d], logit_send.at[0], logit_recv.at[0], device(x, (y + d) % RING, z, core))

    partner = device(x, y, z, 1 - core)
    send(
        gate.at[:, 1 - core], wg.at[:, :, pl.ds(pl.multiple_of(core * LANES, LANES), LANES)],
        weight_send.at[0], weight_recv.at[0], partner,
    )
    send(
        up.at[:, 1 - core], wu.at[:, :, pl.ds(pl.multiple_of(core * LANES, LANES), LANES)],
        weight_send.at[1], weight_recv.at[1], partner,
    )

    @pl.loop(0, 2 * RING)
    def _(block):
        send(down_columns(block, 1 - core), down_rows(block), weight_send.at[2], weight_recv.at[2], partner)

    wait(rx.at[pl.ds(0, 15)], x_recv)
    packed = jnp.where(
        iota((ROWS, LANES), 1) == (iota((ROWS, LANES), 0) // CAP) * SLOT + iota((ROWS, LANES), 0) % CAP, 1.0, 0.0
    ).astype(BF16)
    arrived = rx[...].astype(F32).reshape(2 * RING * SLOT, LANES).astype(BF16)
    xg[0, 0] = jnp.dot(packed, arrived, preferred_element_type=F32).astype(BF16)
    for d in (4, 3, 5, 2, 6, 1, 7):
        send(xg.at[0, 0], xg.at[0, d], first_send, gather_recv.at[0, d], on_plane((a1 + d) % RING, a2))

    def forward(d2, d1, to):
        step = 1 if to < 5 and to > d2 else RING - 1
        send(xg.at[d2, d1], xg.at[to, d1], ring_send, gather_recv.at[to, d1], on_plane(a1, (a2 + step) % RING))

    def multiply(d2, d1):
        oy, oz = turned((a1 + RING - d1) % RING, (a2 + RING - d2) % RING)
        group = oz % 4
        block = (oz // 4) * RING + oy
        piece = xg[d2, d1]
        return group, jnp.dot(piece, wg[block], preferred_element_type=F32), jnp.dot(
            piece, wu[block], preferred_element_type=F32
        )

    def gather_event(level, d1, first=False):
        if level == 0:
            if not first:
                wait(xg.at[0, d1], gather_recv.at[0, d1])
            forward(0, d1, 1)
            forward(0, d1, 7)
            sides = (0,)
        elif level < 4:
            sides = (level, RING - level)
            for side in sides:
                wait(xg.at[side, d1], gather_recv.at[side, d1])
                if level < 3:
                    forward(side, d1, side + 1 if side < 4 else side - 1)
                else:

                    @pl.when(d1 % 2 == (0 if side < 4 else 1))
                    def _(side=side):
                        send(
                            xg.at[side, d1], xg.at[4, d1], ring_send, gather_recv.at[4, d1],
                            on_plane(a1, (a2 + (1 if side < 4 else RING - 1)) % RING),
                        )
        else:
            sides = (4,)
            wait(xg.at[4, d1], gather_recv.at[4, d1])
        products = [multiply(side, d1) for side in sides]
        for group, by_gate, by_up in products:
            acc[group, 0] += by_gate
            acc[group, 1] += by_up

    def outward(k):
        return (k % 2) * ((k + 1) // 2) + (1 - k % 2) * ((RING - k // 2) % RING)

    def weights_there():
        wait(gate.at[:, core], weight_local.at[0])
        wait(up.at[:, core], weight_local.at[1])
        wait(gate.at[:, core], weight_recv.at[0])
        wait(up.at[:, core], weight_recv.at[1])

    forward(0, 0, 1)
    forward(0, 0, 7)
    weights_there()
    group, by_gate, by_up = multiply(0, 0)
    acc[group, 0] += by_gate
    acc[group, 1] += by_up
    for wave in range(5):
        if wave < 4:
            gather_event(wave + 1, 0)

        @pl.loop(1, RING)
        def _(k, wave=wave):
            gather_event(wave, outward(k))

    for g in range(4):
        send(acc.at[g], peer.at[g], swap_send, swap_recv.at[g], partner)

    wait(logit_y.at[pl.ds(0, 7)], logit_recv.at[0])
    logit_z[...] = jnp.sum(logit_y[...], axis=0)
    send(logit_z, logit_far, logit_send.at[1], logit_recv.at[1], device(x, y, (z + 4) % RING, core))

    for g in range(4):
        wait(peer.at[g], swap_recv.at[g])
        by_gate = acc[g, 0] + peer[g, 0]
        by_up = acc[g, 1] + peer[g, 1]
        hid[g] = (by_gate / (1.0 + jnp.exp(-by_gate)) * by_up).astype(BF16)

    wait(wd.at[pl.ds(0, 8)], weight_local.at[2])
    wait(wd.at[pl.ds(0, 8)], weight_recv.at[2])

    def partial(d2, d1):
        ty, tz = turned((a1 + d1) % RING, (a2 + d2 + RING) % RING)
        return jnp.dot(hid[tz % 4], wd[(tz // 4) * RING + ty], preferred_element_type=F32)

    for turn in range(4):

        @pl.loop(0, RING)
        def _(k, turn=turn):
            d1 = outward(RING - 1 - k)
            sign = 1 - 2 * (d1 % 2)
            far = partial(sign * (4 - turn), d1)
            near = partial(-sign * (3 - turn), d1) if turn < 3 else None
            if turn:
                wait(long_in.at[turn - 1, d1], long_recv.at[turn - 1, d1])
                far += long_in[turn - 1, d1].astype(F32)
            long_out[turn, d1] = far.astype(BF16)
            send(
                long_out.at[turn, d1], long_in.at[turn, d1], reduce_send.at[0], long_recv.at[turn, d1],
                on_plane(a1, (a2 + sign + RING) % RING),
            )
            if turn < 3:
                if turn:
                    wait(short_in.at[turn - 1, d1], short_recv.at[turn - 1, d1])
                    near += short_in[turn - 1, d1].astype(F32)
                short_out[turn, d1] = near.astype(BF16)
                send(
                    short_out.at[turn, d1], short_in.at[turn, d1], reduce_send.at[1], short_recv.at[turn, d1],
                    on_plane(a1, (a2 - sign + RING) % RING),
                )

    def reduced(d1):
        own = partial(0, d1)
        wait(long_in.at[3, d1], long_recv.at[3, d1])
        wait(short_in.at[2, d1], short_recv.at[2, d1])
        return own + long_in[3, d1].astype(F32) + short_in[2, d1].astype(F32)

    @pl.loop(0, RING - 1)
    def _(k):
        d1 = outward(RING - 1 - k)
        last_out[d1] = reduced(d1).astype(BF16)
        send(last_out.at[d1], last_in.at[d1], last_send, last_recv.at[d1], on_plane((a1 + d1) % RING, a2))

    fin[...] = reduced(0)

    wait(logit_far, logit_recv.at[1])
    logits = logit_z[...] + logit_far[...]
    signs = jnp.where(lane % RING == r0, 1.0, 0.0) - jnp.where(lane % RING == r1, 1.0, 0.0)
    gap = jnp.sum(jnp.where(own_lanes, signs * logits, 0.0), axis=1, keepdims=True)
    weight = jnp.where(hot0, 1.0 / (1.0 + jnp.exp(-gap)), 1.0 / (1.0 + jnp.exp(gap)))
    combine = (assign * weight)[:, : RING * SLOT]

    total = fin[...]
    for d in (1, 7, 2, 6, 3, 5, 4):
        wait(last_in.at[d], last_recv.at[d])
        total += last_in[d].astype(F32)

    unpacked = jnp.where(
        iota((LANES, ROWS), 0) == (iota((LANES, ROWS), 1) // CAP) * SLOT + iota((LANES, ROWS), 1) % CAP, 1.0, 0.0
    ).astype(BF16)
    opened = jnp.dot(unpacked, total.astype(BF16), preferred_element_type=F32)
    for i in range(2 * RING):
        back_out[i] = opened[i * SLOT : (i + 1) * SLOT].astype(BF16)
    for d in (4, 3, 5, 2, 6, 1, 7, 0):
        i = (x + d) % RING
        send(back_out.at[i * 2 + 1 - core], back_in.at[core, x], back_send, back_recv, device(i, y, z, 1 - core))
        if d:
            send(back_out.at[i * 2 + core], back_in.at[core, x], back_send, back_recv, device(i, y, z, core))
    back_in[core, x] = back_out[me_x]

    wait(tx.at[pl.ds(0, 15)], x_send)
    wait(logit_y.at[pl.ds(0, 7)], logit_send.at[0])
    wait(logit_z, logit_send.at[1])
    wait(gate.at[:, core], weight_send.at[0])
    wait(up.at[:, core], weight_send.at[1])
    wait(wd.at[pl.ds(0, 8)], weight_send.at[2])
    wait(xg.at[0, pl.ds(0, 7)], first_send)
    wait(xg.at[pl.ds(0, 7)], ring_send)
    wait(acc, swap_send)
    wait(long_out, reduce_send.at[0])
    wait(short_out, reduce_send.at[1])
    wait(last_out.at[pl.ds(0, 7)], last_send)

    wait(back_out.at[pl.ds(0, 15)], back_recv)
    for half in range(2):
        pieces = back_in[half].astype(F32).reshape(RING * SLOT, LANES)
        out[:, half * LANES : (half + 1) * LANES] = jnp.dot(
            combine, pieces, precision=lax.Precision.HIGHEST, preferred_element_type=F32
        ).astype(BF16)
    wait(back_out.at[pl.ds(0, 15)], back_send)


def per_device(tokens, routes, router_weight, gate_weight, up_weight, down_weight):
    blocks, width = 2 * RING, 2 * LANES
    dma = pltpu.SemaphoreType.DMA
    vmem = pltpu.VMEM
    in_vmem = pl.BlockSpec(memory_space=pltpu.VMEM)
    in_hbm = pl.BlockSpec(memory_space=pl.ANY)
    return pl.pallas_call(
        kernel,
        out_shape=jax.ShapeDtypeStruct((TOK, width), BF16),
        in_specs=[in_vmem] * 3 + [in_hbm] * 3,
        out_specs=in_vmem,
        scratch_shapes=[
            vmem((blocks, SLOT, LANES), BF16),
            vmem((blocks, SLOT, LANES), BF16),
            vmem((RING, RING, ROWS, LANES), BF16),
            vmem((blocks, LANES, width), BF16),
            vmem((blocks, LANES, width), BF16),
            vmem((blocks, width, LANES), BF16),
            vmem((4, 2, ROWS, width), F32),
            vmem((4, 2, ROWS, width), F32),
            vmem((4, ROWS, width), BF16),
            vmem((4, RING, ROWS, LANES), BF16),
            vmem((3, RING, ROWS, LANES), BF16),
            vmem((4, RING, ROWS, LANES), BF16),
            vmem((3, RING, ROWS, LANES), BF16),
            vmem((RING, ROWS, LANES), BF16),
            vmem((RING, ROWS, LANES), BF16),
            vmem((blocks, SLOT, LANES), BF16),
            vmem((2, RING, SLOT, LANES), BF16),
            vmem((ROWS, LANES), F32),
            vmem((RING, 1, LANES), F32),
            vmem((1, LANES), F32),
            vmem((1, LANES), F32),
            dma((3,)),
            dma((3,)),
            dma((3,)),
            dma,
            dma,
            dma,
            dma,
            dma((RING, RING)),
            dma((2,)),
            dma((2,)),
            dma,
            dma((4,)),
            dma((2,)),
            dma((4, RING)),
            dma((3, RING)),
            dma,
            dma((RING,)),
            dma,
            dma,
        ],
        compiler_params=pltpu.CompilerParams(collective_id=0, has_side_effects=True),
        name="moe",
    )(
        tokens,
        routes,
        router_weight,
        gate_weight.reshape(blocks, 2, LANES, LANES),
        up_weight.reshape(blocks, 2, LANES, LANES),
        down_weight[0],
    )


def solution(mesh):
    return jax.shard_map(
        per_device,
        mesh=mesh,
        in_specs=(
            P(("expert", "dp"), "mp"),
            P(("expert", "dp"), None),
            P("mp", None),
            P("expert", None, ("dp", "mp")),
            P("expert", None, ("dp", "mp")),
            P("expert", ("dp", "mp"), None),
        ),
        out_specs=P(("expert", "dp"), "mp"),
        check_vma=False,
    )
```

time: 272 us -> 78.4 us (0.29)
  waiting for transfers between devices: 157 us -> 0 us
  Pallas kernels: 0 us -> 74.8 us
  blocking collectives: 49.2 us -> 0 us
  starting transfers between devices: 30.3 us -> 0 us
  between operations: 13.5 us -> 0.01 us
  matrix products: 11.4 us -> 0 us
  local copies, waits for them, and re-layouts: 6.47 us -> 3.38 us
    pallas_call x0 -> x1, Pallas kernels: none -> 74.8 us  [per_device(): pl.pallas_call(kernel, out_shape=jax.ShapeDtypeStruct((TOK, width), BF16)...]
    reduce_scatter x1 -> x0, waiting for transfers between devices: 69.3 us -> none  [per_device(): lax.psum_scatter(jnp.dot(hidden, down_weight[0], preferred_element_type=j...]
    all_to_all x2 -> x0, blocking collectives: 49.2 us -> none  [the longest x1 29.8 us: summed_on_arrival(): pieces = lax.all_to_all(in_blocks(x, dim, length), axis, 0, 0, tiled=True)]
    all_to_all x3 -> x0, waiting for transfers between devices: 45.6 us -> none  [the longest x1 25.7 us: per_device(): lax.all_to_all(summed.reshape(experts, capacity, full_width), 'expert', s...]
    all_gather x1 -> x0, waiting for transfers between devices: 42.5 us -> none  [per_device(): lax.all_gather(arrived.reshape(experts * capacity, full_width), 'dp', axi...]
    all_to_all x3 -> x0, starting transfers between devices: 30.2 us -> none  [the longest x2 23.8 us: from_everyone(): lax.all_to_all(jnp.broadcast_to(x[None], (length, *x.shape)), axis, 0, 0,...]
    dot_general x5 -> x0, matrix products: 11.4 us -> none  [the longest x1 6.95 us: per_device(): jnp.dot(hidden, down_weight[0], preferred_element_type=jnp.float32)]
    reshape x5 -> x0, local copies, waits for them, and re-layouts: 3.24 us -> none  [the longest x1 2.18 us: per_device(): summed.reshape(experts, capacity, full_width)]
  transfers between devices with their start and end apart: 5 -> 0, of which waited for: 5 -> 0; matrix products, arithmetic and copies ran while one was open for 1% -> 0% of each run, Pallas kernels for 0% -> 0%
where the time goes in v1:
time: 78.4 us; the launch traced here: 78.2 us
  Pallas kernels  74.8 us (95%)
  local copies, waits for them, and re-layouts  3.38 us (4%)
    pallas_call x1, Pallas kernels, per_device(): pl.pallas_call(kernel, out_shape=jax.ShapeDtypeStruct((TOK, width), BF16)...  74.8 us
    unnamed x7, local copies, waits for them, and re-layouts  3.38 us

profile of v1, /device:TPU:1, one launch (start us, length us, event | category | flops | bytes accessed | tf_op | source)
XLA Modules:
  0.0 78.2 jit_solution(11150616385591850278)
XLA Ops:
  0.0 0.0 copy-start.1
  0.0 0.7 copy-done.1
  0.7 0.0 copy-start
  0.7 0.7 copy.7.routes
  1.4 0.0 copy-done
  1.4 0.7 copy.8.router
  2.1 74.8 %moe.1 = bf16[12,256]{1,0:T(8,128)(2,1)} custom-call(bf16[12,256]{1,0:T(8,128)(2,1)} %tokens.1, s32[12,2]{1,0:T(8,128)} %copy.7.routes, bf16[256,8]{1,0:T(8,128)(2,1)} %copy.8.router, bf16[16,2,128,128]{3,2,1,0:T(8,128)(2,1)} %bitcast.3, bf16[16,2,128,128]{3,2,1,0:T(8,128)(2,1)} %bitcast.4, bf16[128,4096]{1,0:T(8,128)(2,1)} %bitcast.5), custom_call_target="tpu_custom_call" | custom-call | tf_op jit(solution)/shard_map/moe/pallas_call | solution.py:327
  76.9 1.3 %copy.10 = bf16[12,256]{1,0:T(8,128)(2,1)} copy(bf16[12,256]{1,0:T(8,128)(2,1)} %moe.1) | data formatting | bytes 12288
Async XLA Ops:
  0.0 0.7 copy-start.1
  0.7 0.7 copy-start

commit v2 on v1

v2 whole, which is shorter than its diff:
```python
import jax
import jax.numpy as jnp
from jax import lax
from jax.experimental import pallas as pl
from jax.experimental.pallas import tpu as pltpu
from jax.sharding import PartitionSpec as P

MESH = pl.DeviceIdType.MESH
F32 = jnp.float32
BF16 = jnp.bfloat16
RING = 8
TOK = 12
CAP = 5
SLOT = 8
ROWS = 2 * RING * CAP
LANES = 128


def iota(shape, dim):
    return lax.broadcasted_iota(jnp.int32, shape, dim)


def kernel(
    tokens, routes, router, gate, up, down, out,
    tx, rx, xg, wg, wu, wd_z, wd_y, acc, peer, hid, part, reduce_out, reduce_in,
    last_out, last_in, back_out, back_in, fin, router_here, logit_y, logit_z, logit_far,
    weight_local, weight_send, weight_recv, x_send, x_recv, first_send, first_recv, ring_send, pair_recv, batch_recv,
    logit_send, logit_recv, swap_send, swap_recv, reduce_send, reduce_recv,
    last_send, last_recv, back_send, back_recv,
):
    x = lax.axis_index("expert")
    dp = lax.axis_index("dp")
    mp = lax.axis_index("mp")
    core = dp % 2
    z = (mp // RING) * 4 + dp // 2
    y = mp % RING
    a1 = (1 - core) * y + core * z
    a2 = (1 - core) * z + core * y

    def device(dx, dy, dz, dcore):
        return (dx, (dz % 4) * 2 + dcore, (dz // 4) * RING + dy)

    def on_plane(b1, b2):
        return device(x, (1 - core) * b1 + core * b2, (1 - core) * b2 + core * b1, core)

    def send(src, dst, send_sem, recv_sem, target):
        pltpu.make_async_remote_copy(
            src_ref=src, dst_ref=dst, send_sem=send_sem, recv_sem=recv_sem,
            device_id=target, device_id_type=MESH,
        ).start()

    def wait(ref, sem):
        pltpu.make_async_copy(ref, ref, sem).wait()

    def outward(k):
        return (k % 2) * ((k + 1) // 2) + (1 - k % 2) * ((RING - k // 2) % RING)

    def near_first(k):
        return (a1 + outward(k)) % RING

    def far_first(k):
        return (a1 + outward(RING - 1 - k)) % RING

    barrier = pltpu.get_barrier_semaphore()

    def greet(target):
        pl.semaphore_signal(barrier, inc=1, device_id=target, device_id_type=MESH)

    for d in (4, 3, 5, 2, 6, 1, 7):
        greet(device((x + d) % RING, y, z, core))
        greet(device((x + d) % RING, y, z, 1 - core))
        greet(device(x, (y + d) % RING, z, core))
        greet(device(x, y, (z + d) % RING, core))
    greet(device(x, y, z, 1 - core))

    pltpu.make_async_copy(router, router_here, weight_local.at[3]).start()

    r0 = routes[0:1, :]
    r1 = routes[1:2, :]
    row = iota((RING * SLOT, TOK), 0)
    hot0 = r0 == row // SLOT
    hot = jnp.where(hot0 | (r1 == row // SLOT), 1.0, 0.0)
    earlier = jnp.where(iota((TOK, TOK), 0) < iota((TOK, TOK), 1), 1.0, 0.0)
    before = jnp.dot(hot.astype(BF16), earlier.astype(BF16), preferred_element_type=F32)
    assign = jnp.where(before == (row % SLOT).astype(F32), hot, 0.0)
    tok = tokens[...]
    chosen = jnp.dot(assign.astype(BF16), tok, preferred_element_type=F32)
    for e in range(RING):
        for half in range(2):
            tx[e * 2 + half] = chosen[
                e * SLOT : (e + 1) * SLOT, half * LANES : (half + 1) * LANES
            ].astype(BF16)
    me_x = x * 2 + core
    rx[me_x] = tx[me_x]

    pl.semaphore_wait(barrier, 4 * (RING - 1) + 1)

    for d in (4, 3, 5, 2, 6, 1, 7, 0):
        e = (x + d) % RING
        send(tx.at[e * 2 + 1 - core], rx.at[me_x], x_send, x_recv, device(e, y, z, 1 - core))
        if d:
            send(tx.at[e * 2 + core], rx.at[me_x], x_send, x_recv, device(e, y, z, core))

    partner = device(x, y, z, 1 - core)
    units = pl.ds(pl.multiple_of(core * LANES, LANES), LANES)

    def down_columns(block, half):
        return down.at[:, pl.ds(pl.multiple_of((block * 2 + half) * LANES, LANES), LANES)]

    @pl.loop(0, 2 * RING)
    def _(block):
        high, wy = block // RING, block % RING
        for half in range(2):
            place = block if half == 0 else wy * 2 + high
            if half == 0:
                down_place = wd_z.at[high, units, pl.ds(pl.multiple_of(wy * LANES, LANES), LANES)]
            else:
                down_place = wd_y.at[wy, units, pl.ds(pl.multiple_of(high * LANES, LANES), LANES)]
            moves = (
                (gate.at[block, half], wg.at[place, :, units]),
                (up.at[block, half], wu.at[place, :, units]),
                (down_columns(block, half), down_place),
            )

            @pl.when(core == half)
            def _(moves=moves):
                for i, (src, dst) in enumerate(moves):
                    pltpu.make_async_copy(src, dst, weight_local.at[i]).start()

            @pl.when(core != half)
            def _(moves=moves):
                for i, (src, dst) in enumerate(moves):
                    send(src, dst, weight_send.at[i], weight_recv.at[i], partner)

    own_lanes = iota((RING, LANES), 1) % RING == iota((RING, LANES), 0)
    of_token = jnp.where(iota((TOK, LANES), 1) // RING == iota((TOK, LANES), 0), 1.0, 0.0)
    wait(router_here, weight_local.at[3])
    term = lax.dot_general(router_here[...], tok, (((1,), (1,)), ((), ())), preferred_element_type=F32)
    wide = jnp.dot(term, of_token, precision=lax.Precision.HIGHEST, preferred_element_type=F32)
    logit_y[0] = jnp.sum(jnp.where(own_lanes, wide, 0.0), axis=0, keepdims=True)
    for d in (4, 3, 5, 2, 6, 1, 7):
        send(logit_y.at[0], logit_y.at[d], logit_send.at[0], logit_recv.at[0], device(x, (y + d) % RING, z, core))
    acc[...] = jnp.zeros_like(acc)
    packed = jnp.where(
        iota((ROWS, LANES), 1) == (iota((ROWS, LANES), 0) // CAP) * SLOT + iota((ROWS, LANES), 0) % CAP, 1.0, 0.0
    ).astype(BF16)

    wait(rx.at[pl.ds(0, 15)], x_recv)
    arrived = rx[...].astype(F32).reshape(2 * RING * SLOT, LANES).astype(BF16)
    xg[0, a1] = jnp.dot(packed, arrived, preferred_element_type=F32).astype(BF16)
    for d in (1, 7, 2, 6, 3, 5, 4):
        send(xg.at[0, a1], xg.at[0, a1], first_send, first_recv.at[a1], on_plane((a1 + d) % RING, a2))

    def along(d2, j, to, hop, sem):
        send(xg.at[d2, j], xg.at[to, j], ring_send, sem, on_plane(a1, (a2 + hop + RING) % RING))

    def to_second(j):
        along(0, j, 2, 2, pair_recv.at[j])
        along(0, j, 6, -2, pair_recv.at[j])

    def to_next(j):
        along(0, j, 1, 1, batch_recv.at[1])
        along(0, j, 7, -1, batch_recv.at[7])

    def from_second(j):
        wait(xg.at[pl.ds(0, 2), j], pair_recv.at[j])
        for i, (at, sign) in enumerate(((2, 1), (6, -1))):

            @pl.when(j % 2 == i)
            def _(at=at, sign=sign):
                along(at, j, 4, 2 * sign, batch_recv.at[4])

            along(at, j, at + sign, sign, batch_recv.at[at + sign])

    def multiply(d2):
        origin = (a2 + RING - d2) % RING

        @pl.when(core == 0)
        def _():
            rows = jnp.concatenate([xg[d2, j] for j in range(RING)], axis=1)
            group, first = origin % 4, (origin // 4) * RING
            for i, w in enumerate((wg, wu)):
                acc[group, i] += jnp.dot(
                    rows, w[pl.ds(first, RING)].reshape(RING * LANES, 2 * LANES), preferred_element_type=F32
                )

        @pl.when(core == 1)
        def _():
            rows = jnp.concatenate(
                [xg[d2, 0:4].reshape(4 * ROWS, LANES), xg[d2, 4:8].reshape(4 * ROWS, LANES)], axis=1
            )
            for i, w in enumerate((wg, wu)):
                acc[:, i] += jnp.dot(
                    rows, w[pl.ds(origin * 2, 2)].reshape(2 * LANES, 2 * LANES), preferred_element_type=F32
                ).reshape(4, ROWS, 2 * LANES)

    def first_event(k):
        j = near_first(k)
        wait(xg.at[0, j], first_recv.at[j])
        to_second(j)

    to_second(a1)
    to_next(a1)
    first_event(1)
    first_event(2)
    from_second(a1)

    @pl.loop(3, RING)
    def _(k):
        first_event(k)

    for i in range(2):
        wait(wg.at[pl.ds(0, 8)], (weight_local, weight_recv)[i].at[0])
        wait(wu.at[pl.ds(0, 8)], (weight_local, weight_recv)[i].at[1])
    multiply(0)

    @pl.loop(1, 5)
    def _(k):
        to_next(near_first(k))

    @pl.loop(1, RING)
    def _(k):
        from_second(near_first(k))

        @pl.when(k > 4)
        def _():
            to_next(near_first(k))

    def swap(g):
        send(acc.at[g], peer.at[g], swap_send, swap_recv.at[g], partner)

    def swap_done(d2):
        @pl.when(core == 0)
        def _():
            swap((a2 + RING - d2) % 4)

    multiply(2)
    multiply(6)
    swap_done(2)
    for d2 in (1, 7, 3, 5, 4):
        wait(xg.at[d2], batch_recv.at[d2])
        multiply(d2)
        if d2 in (3, 5, 4):
            swap_done(d2)

    @pl.when(core == 1)
    def _():
        for g in range(4):
            swap(g)

    wait(logit_y.at[pl.ds(0, 7)], logit_recv.at[0])
    logit_z[...] = jnp.sum(logit_y[...], axis=0)
    send(logit_z, logit_far, logit_send.at[1], logit_recv.at[1], device(x, y, (z + 4) % RING, core))
    for i in range(2):
        wait(wd_z.at[0], (weight_local, weight_recv)[i].at[2])

    for g in range(4):
        wait(peer.at[g], swap_recv.at[g])
        by_gate = acc[g, 0] + peer[g, 0]
        by_up = acc[g, 1] + peer[g, 1]
        hid[g] = (by_gate / (1.0 + jnp.exp(-by_gate)) * by_up).astype(BF16)

    def partial(d2, put):
        target = (a2 + d2 + RING) % RING

        @pl.when(core == 0)
        def _():
            terms = jnp.dot(hid[target % 4], wd_z[target // 4], preferred_element_type=F32)
            for j in range(RING):
                put(j, terms[:, j * LANES : (j + 1) * LANES])

        @pl.when(core == 1)
        def _():
            terms = jnp.dot(hid[...].reshape(4 * ROWS, 2 * LANES), wd_y[target], preferred_element_type=F32)
            for j in range(RING):
                low, high = j % 4, j // 4
                put(j, terms[low * ROWS : (low + 1) * ROWS, high * LANES : (high + 1) * LANES])

    def hop_on(m, j, hop):
        send(
            reduce_out.at[m, j], reduce_in.at[m, j], reduce_send, reduce_recv.at[m // 3 - m // 6, j],
            on_plane(a1, (a2 + hop + RING) % RING),
        )

    def put_out(m):
        def put(j, value):
            reduce_out[m, j] = value.astype(BF16)

        return put

    def put_part(i):
        def put(j, value):
            part[i, j] = value

        return put

    partial(4, put_out(0))

    @pl.loop(0, RING)
    def _(k):
        j = far_first(k)
        hop_on(0, j, 2 - 4 * (j % 2))

    for m, d2, hop in ((1, 3, 1), (2, -3, -1), (3, 1, 1), (4, -1, -1)):
        partial(d2, put_out(m))

        @pl.loop(0, RING)
        def _(k, m=m, hop=hop):
            hop_on(m, far_first(k), hop)

    partial(2, put_part(0))
    partial(-2, put_part(1))

    @pl.loop(0, RING)
    def _(k):
        j = far_first(k)
        wait(reduce_in.at[pl.ds(0, 3), j], reduce_recv.at[0, j])
        fourth = reduce_in[0, j].astype(F32)
        even = j % 2 == 0
        ahead = part[0, j] + reduce_in[1, j].astype(F32) + jnp.where(even, fourth, 0.0)
        behind = part[1, j] + reduce_in[2, j].astype(F32) + jnp.where(even, 0.0, fourth)
        reduce_out[5, j] = ahead.astype(BF16)
        hop_on(5, j, 2)
        reduce_out[6, j] = behind.astype(BF16)
        hop_on(6, j, -2)

    partial(0, put_part(2))

    def reduced(j):
        total = part[2, j]
        wait(reduce_in.at[pl.ds(3, 4), j], reduce_recv.at[1, j])
        for m in range(3, 7):
            total += reduce_in[m, j].astype(F32)
        return total

    @pl.loop(0, RING - 1)
    def _(k):
        j = far_first(k)
        last_out[j] = reduced(j).astype(BF16)
        send(last_out.at[j], last_in.at[a1], last_send, last_recv, on_plane(j, a2))

    fin[...] = reduced(a1)

    wait(logit_far, logit_recv.at[1])
    logits = jnp.where(own_lanes, logit_z[...] + logit_far[...], 0.0)
    logits = lax.dot_general(
        logits, of_token, (((1,), (1,)), ((), ())), precision=lax.Precision.HIGHEST, preferred_element_type=F32
    )
    expert = iota((RING, TOK), 0)
    gap = jnp.sum(jnp.where(r0 == expert, logits, 0.0) - jnp.where(r1 == expert, logits, 0.0), axis=0, keepdims=True)
    combine = assign * jnp.where(hot0, 1.0 / (1.0 + jnp.exp(-gap)), 1.0 / (1.0 + jnp.exp(gap)))
    unpacked = jnp.where(
        iota((LANES, ROWS), 0) == (iota((LANES, ROWS), 1) // CAP) * SLOT + iota((LANES, ROWS), 1) % CAP, 1.0, 0.0
    ).astype(BF16)

    total = fin[...]
    wait(last_in.at[pl.ds(0, 7)], last_recv)
    for d in range(1, RING):
        total += last_in[(a1 + d) % RING].astype(F32)

    opened = jnp.dot(unpacked, total.astype(BF16), preferred_element_type=F32)
    for i in range(2 * RING):
        back_out[i] = opened[i * SLOT : (i + 1) * SLOT].astype(BF16)
    for d in (4, 3, 5, 2, 6, 1, 7, 0):
        i = (x + d) % RING
        send(back_out.at[i * 2 + 1 - core], back_in.at[core, x], back_send, back_recv, device(i, y, z, 1 - core))
        if d:
            send(back_out.at[i * 2 + core], back_in.at[core, x], back_send, back_recv, device(i, y, z, core))
    back_in[core, x] = back_out[me_x]

    wait(tx.at[pl.ds(0, 15)], x_send)
    wait(logit_y.at[pl.ds(0, 7)], logit_send.at[0])
    wait(logit_z, logit_send.at[1])
    wait(wg.at[pl.ds(0, 8)], weight_send.at[0])
    wait(wu.at[pl.ds(0, 8)], weight_send.at[1])
    wait(wd_z.at[0], weight_send.at[2])
    wait(xg.at[0, pl.ds(0, 7)], first_send)
    wait(xg.at[pl.ds(0, 7)], ring_send)
    wait(acc, swap_send)
    wait(reduce_out, reduce_send)
    wait(last_out.at[pl.ds(0, 7)], last_send)

    wait(back_out.at[pl.ds(0, 15)], back_recv)
    for half in range(2):
        pieces = back_in[half].astype(F32).reshape(RING * SLOT, LANES)
        out[:, half * LANES : (half + 1) * LANES] = lax.dot_general(
            combine, pieces, (((0,), (0,)), ((), ())), precision=lax.Precision.HIGHEST, preferred_element_type=F32
        ).astype(BF16)
    wait(back_out.at[pl.ds(0, 15)], back_send)


def per_device(tokens, routes, router_weight, gate_weight, up_weight, down_weight):
    blocks, width = 2 * RING, 2 * LANES
    dma = pltpu.SemaphoreType.DMA
    vmem = pltpu.VMEM
    in_vmem = pl.BlockSpec(memory_space=pltpu.VMEM)
    in_hbm = pl.BlockSpec(memory_space=pltpu.HBM)
    return pl.pallas_call(
        kernel,
        out_shape=jax.ShapeDtypeStruct((TOK, width), BF16),
        in_specs=[in_vmem] * 2 + [in_hbm] * 4,
        out_specs=in_vmem,
        scratch_shapes=[
            vmem((blocks, SLOT, LANES), BF16),
            vmem((blocks, SLOT, LANES), BF16),
            vmem((RING, RING, ROWS, LANES), BF16),
            vmem((blocks, LANES, width), BF16),
            vmem((blocks, LANES, width), BF16),
            vmem((2, width, RING * LANES), BF16),
            vmem((RING, width, width), BF16),
            vmem((4, 2, ROWS, width), F32),
            vmem((4, 2, ROWS, width), F32),
            vmem((4, ROWS, width), BF16),
            vmem((3, RING, ROWS, LANES), F32),
            vmem((7, RING, ROWS, LANES), BF16),
            vmem((7, RING, ROWS, LANES), BF16),
            vmem((RING, ROWS, LANES), BF16),
            vmem((RING, ROWS, LANES), BF16),
            vmem((blocks, SLOT, LANES), BF16),
            vmem((2, RING, SLOT, LANES), BF16),
            vmem((ROWS, LANES), F32),
            vmem((RING, width), BF16),
            vmem((RING, 1, LANES), F32),
            vmem((1, LANES), F32),
            vmem((1, LANES), F32),
            dma((4,)),
            dma((3,)),
            dma((3,)),
            dma,
            dma,
            dma,
            dma((RING,)),
            dma,
            dma((RING,)),
            dma((RING,)),
            dma((2,)),
            dma((2,)),
            dma,
            dma((4,)),
            dma,
            dma((2, RING)),
            dma,
            dma,
            dma,
            dma,
        ],
        compiler_params=pltpu.CompilerParams(collective_id=0, has_side_effects=True, vmem_limit_bytes=40 * 2**20),
        name="moe",
    )(
        tokens,
        routes.T,
        *(
            pltpu.with_memory_space_constraint(w, pltpu.HBM)
            for w in (
                router_weight.T,
                gate_weight.reshape(blocks, 2, LANES, LANES),
                up_weight.reshape(blocks, 2, LANES, LANES),
                down_weight[0],
            )
        ),
    )


def solution(mesh):
    return jax.shard_map(
        per_device,
        mesh=mesh,
        in_specs=(
            P(("expert", "dp"), "mp"),
            P(("expert", "dp"), None),
            P("mp", None),
            P("expert", None, ("dp", "mp")),
            P("expert", None, ("dp", "mp")),
            P("expert", ("dp", "mp"), None),
        ),
        out_specs=P(("expert", "dp"), "mp"),
        check_vma=False,
    )
```

time: 78.4 us -> 67.4 us (0.86)
  Pallas kernels: 74.8 us -> 65.9 us
  local copies, waits for them, and re-layouts: 3.38 us -> 1.3 us
    pallas_call x1, Pallas kernels: 74.8 us -> 65.9 us  [per_device(): pl.pallas_call(kernel, out_shape=jax.ShapeDtypeStruct((TOK, width), BF16)...]
    unnamed x7 -> x5, local copies, waits for them, and re-layouts: 3.38 us -> 1.3 us
where the time goes in v2:
time: 67.4 us; the launch traced here: 67.2 us
  Pallas kernels  65.9 us (98%)
  local copies, waits for them, and re-layouts  1.3 us (2%)
    pallas_call x1, Pallas kernels, per_device(): pl.pallas_call(kernel, out_shape=jax.ShapeDtypeStruct((TOK, width), BF16)...  65.9 us

profile of v2, /device:TPU:1, one launch (start us, length us, event | category | flops | bytes accessed | tf_op | source)
XLA Modules:
  0.0 67.2 jit_solution(10400873201067029721)
XLA Ops:
  0.0 0.0 copy-start
  0.0 0.0 copy-start.1
  0.0 0.7 %copy-done = bf16[12,256]{1,0:T(8,128)(2,1)S(1)} copy-done((bf16[12,256]{1,0:T(8,128)(2,1)S(1)}, bf16[12,256]{1,0:T(8,128)(2,1)}, u32[]{:S(2)}) %copy-start) | copy-done | bytes 6168
  0.7 0.0 copy-done.1
  0.7 65.9 %moe.1 = bf16[12,256]{1,0:T(8,128)(2,1)S(1)} custom-call(bf16[12,256]{1,0:T(8,128)(2,1)S(1)} %copy-done, s32[2,12]{1,0:T(2,128)S(1)} %bitcast.5, bf16[8,256]{1,0:T(8,128)(2,1)} %bitcast.9, bf16[16,2,128,128]{3,2,1,0:T(8,128)(2,1)} %bitcast.6, bf16[16,2,128,128]{3,2,1,0:T(8,128)(2,1)} %bitcast.7, bf16[128,4096]{1,0:T(8,128)(2,1)} %bitcast.8), custom_call_target="tpu_custom_call" | custom-call | tf_op jit(solution)/shard_map/moe/pallas_call | solution.py:398
  66.6 0.6 copy.8
Async XLA Ops:
  0.0 0.7 %copy-start = (bf16[12,256]{1,0:T(8,128)(2,1)S(1)}, bf16[12,256]{1,0:T(8,128)(2,1)}, u32[]{:S(2)}) copy-start(bf16[12,256]{1,0:T(8,128)(2,1)} %tokens.1) | copy-start | bytes 18436
  0.0 0.7 %copy-start.1 = (s32[12,2]{0,1:T(2,128)S(1)}, s32[12,2]{0,1:T(2,128)}, u32[]{:S(2)}) copy-start(s32[12,2]{0,1:T(2,128)} %param.7) | copy-start | bytes 292

commit v3 on v2

--- a/solution.py
+++ b/solution.py
@@ -23,7 +23,7 @@
 def kernel(
     tokens, routes, router, gate, up, down, out,
     tx, rx, xg, wg, wu, wd_z, wd_y, acc, peer, hid, part, reduce_out, reduce_in,
-    last_out, last_in, back_out, back_in, fin, router_here, logit_y, logit_z, logit_far,
+    last_out, last_in, back_out, back_in, fin, tokens_here, routes_here, router_here, logit_y, logit_z, logit_far,
     weight_local, weight_send, weight_recv, x_send, x_recv, first_send, first_recv, ring_send, pair_recv, batch_recv,
     logit_send, logit_recv, swap_send, swap_recv, reduce_send, reduce_recv,
     last_send, last_recv, back_send, back_recv,
@@ -61,6 +61,10 @@
     def far_first(k):
         return (a1 + outward(RING - 1 - k)) % RING
 
+    small = ((routes, routes_here), (tokens, tokens_here), (router, router_here))
+    small = [pltpu.make_async_copy(*pair, weight_local.at[3 + i]) for i, pair in enumerate(small)]
+    for copy in small:
+        copy.start()
     barrier = pltpu.get_barrier_semaphore()
 
     def greet(target):
@@ -73,17 +77,17 @@
         greet(device(x, y, (z + d) % RING, core))
     greet(device(x, y, z, 1 - core))
 
-    pltpu.make_async_copy(router, router_here, weight_local.at[3]).start()
-
-    r0 = routes[0:1, :]
-    r1 = routes[1:2, :]
+    small[0].wait()
+    r0 = routes_here[0:1, :]
+    r1 = routes_here[1:2, :]
     row = iota((RING * SLOT, TOK), 0)
     hot0 = r0 == row // SLOT
     hot = jnp.where(hot0 | (r1 == row // SLOT), 1.0, 0.0)
     earlier = jnp.where(iota((TOK, TOK), 0) < iota((TOK, TOK), 1), 1.0, 0.0)
     before = jnp.dot(hot.astype(BF16), earlier.astype(BF16), preferred_element_type=F32)
     assign = jnp.where(before == (row % SLOT).astype(F32), hot, 0.0)
-    tok = tokens[...]
+    small[1].wait()
+    tok = tokens_here[...]
     chosen = jnp.dot(assign.astype(BF16), tok, preferred_element_type=F32)
     for e in range(RING):
         for half in range(2):
@@ -134,7 +138,7 @@
 
     own_lanes = iota((RING, LANES), 1) % RING == iota((RING, LANES), 0)
     of_token = jnp.where(iota((TOK, LANES), 1) // RING == iota((TOK, LANES), 0), 1.0, 0.0)
-    wait(router_here, weight_local.at[3])
+    small[2].wait()
     term = lax.dot_general(router_here[...], tok, (((1,), (1,)), ((), ())), preferred_element_type=F32)
     wide = jnp.dot(term, of_token, precision=lax.Precision.HIGHEST, preferred_element_type=F32)
     logit_y[0] = jnp.sum(jnp.where(own_lanes, wide, 0.0), axis=0, keepdims=True)
@@ -209,22 +213,18 @@
     def _(k):
         first_event(k)
 
+    @pl.loop(1, RING)
+    def _(k):
+        to_next(near_first(k))
+
     for i in range(2):
         wait(wg.at[pl.ds(0, 8)], (weight_local, weight_recv)[i].at[0])
         wait(wu.at[pl.ds(0, 8)], (weight_local, weight_recv)[i].at[1])
     multiply(0)
 
-    @pl.loop(1, 5)
-    def _(k):
-        to_next(near_first(k))
-
     @pl.loop(1, RING)
     def _(k):
         from_second(near_first(k))
-
-        @pl.when(k > 4)
-        def _():
-            to_next(near_first(k))
 
     def swap(g):
         send(acc.at[g], peer.at[g], swap_send, swap_recv.at[g], partner)
@@ -398,7 +398,7 @@
     return pl.pallas_call(
         kernel,
         out_shape=jax.ShapeDtypeStruct((TOK, width), BF16),
-        in_specs=[in_vmem] * 2 + [in_hbm] * 4,
+        in_specs=[in_hbm] * 6,
         out_specs=in_vmem,
         scratch_shapes=[
             vmem((blocks, SLOT, LANES), BF16),
@@ -419,11 +419,13 @@
             vmem((blocks, SLOT, LANES), BF16),
             vmem((2, RING, SLOT, LANES), BF16),
             vmem((ROWS, LANES), F32),
+            vmem((TOK, width), BF16),
+            vmem((2, TOK), jnp.int32),
             vmem((RING, width), BF16),
             vmem((RING, 1, LANES), F32),
             vmem((1, LANES), F32),
             vmem((1, LANES), F32),
-            dma((4,)),
+            dma((6,)),
             dma((3,)),
             dma((3,)),
             dma,
@@ -447,11 +449,11 @@
         compiler_params=pltpu.CompilerParams(collective_id=0, has_side_effects=True, vmem_limit_bytes=40 * 2**20),
         name="moe",
     )(
-        tokens,
-        routes.T,
         *(
             pltpu.with_memory_space_constraint(w, pltpu.HBM)
             for w in (
+                tokens,
+                routes.T,
                 router_weight.T,
                 gate_weight.reshape(blocks, 2, LANES, LANES),
                 up_weight.reshape(blocks, 2, LANES, LANES),

time: 67.4 us -> 65.4 us (0.970)
  Pallas kernels: 65.9 us -> 64.6 us
  local copies, waits for them, and re-layouts: 1.3 us -> 0.6 us
    pallas_call x1, Pallas kernels: 65.9 us -> 64.6 us  [per_device(): pl.pallas_call(kernel, out_shape=jax.ShapeDtypeStruct((TOK, width), BF16)...]
    unnamed x5 -> x1, local copies, waits for them, and re-layouts: 1.3 us -> 0.6 us
where the time goes in v3:
time: 65.4 us; the launch traced here: 65.2 us
  Pallas kernels  64.6 us (99%)
    pallas_call x1, Pallas kernels, per_device(): pl.pallas_call(kernel, out_shape=jax.ShapeDtypeStruct((TOK, width), BF16)...  64.6 us

profile of v3, /device:TPU:1, one launch (start us, length us, event | category | flops | bytes accessed | tf_op | source)
XLA Modules:
  0.0 65.2 jit_solution(12698999694461811841)
XLA Ops:
  0.0 64.6 %moe.1 = bf16[12,256]{1,0:T(8,128)(2,1)S(1)} custom-call(bf16[12,256]{1,0:T(8,128)(2,1)} %tokens.1, s32[2,12]{1,0:T(2,128)} %bitcast.9, bf16[8,256]{1,0:T(8,128)(2,1)} %bitcast.8, bf16[16,2,128,128]{3,2,1,0:T(8,128)(2,1)} %bitcast.5, bf16[16,2,128,128]{3,2,1,0:T(8,128)(2,1)} %bitcast.6, bf16[128,4096]{1,0:T(8,128)(2,1)} %bitcast.7), custom_call_target="tpu_custom_call" | custom-call | tf_op jit(solution)/shard_map/moe/pallas_call | solution.py:398
  64.6 0.6 copy.8
